TPU v7x, 32 devices: a whole 2x2x4 slice. The times are simulated.
32 devices in a mesh: grp: 2 (over x), panel: 16 (over z, y, core).
Axes of the slice: x: 2, y: 2, z: 4, core: 2. Of those that a mesh axis runs over, the one named last changes fastest.
Arguments:
- density: bfloat16 [1024, 16, 128], P(('grp', 'panel')), parts along dimension 0, may hold values from -6 to 6
- near_blocks: bfloat16 [1024, 8, 128, 128], P(('grp', 'panel')), parts along dimension 0, may hold values from -0.1875 to 0.1875
- neighbours: int32 [1024, 8], P(('grp', 'panel')), parts along dimension 0, may hold values from 0 to 511, as said below
- counts: int32 [1024], P(('grp', 'panel')), parts along dimension 0, may hold values from 1 to 8, as said below
- coarse_map: int32 [1024], P(('grp', 'panel')), parts along dimension 0, may hold values from 0 to 31, as said below
- restrict: bfloat16 [1024, 128, 128], P(('grp', 'panel')), parts along dimension 0, may hold values from -0.125 to 0.125
- evaluate: bfloat16 [1024, 128, 128], P(('grp', 'panel')), parts along dimension 0, may hold values from -0.5 to 0.5
- coupling: float32 [64, 32], P(('grp', 'panel')), parts along dimension 0, as said below
Outputs:
- potential: bfloat16 [1024, 16, 128], P(('grp', 'panel')), parts along dimension 0
There are 2 independent parts, one for each index of `grp`. A program takes and returns all parts, laid end to end along the dimension named above; each array names one. Nothing has to cross between parts.
Inputs may be any that keep to these rules, and one draw needn't show every extreme that they name: `neighbours`: slot 0 of block b is b itself; every entry lies within 16 blocks of b; in every draw some entry lies exactly 16 blocks below its block and some exactly 16 above. `counts`: every device holds blocks with all 8 slots live. `coarse_map`: block b's coarse cluster is one of the 2 clusters from (b // 32) * 2 on. `coupling`: the matrix is symmetric.
All inputs are finite; a program needn't handle non-finite values.
Results may differ from a plain program's by a relative error of at most 0.0042.
Values may be sent and summed in bfloat16 or wider, within the bound.
A program may use at most 64 MiB of HBM per device.

v0:
```python
import functools

import jax
import jax.numpy as jnp
from jax import lax
from jax.experimental import pallas as pl
from jax.experimental.pallas import tpu as pltpu
from jax.sharding import PartitionSpec as P

CHUNK = 8
CONTRACT_LAST = (((1,), (1,)), ((), ()))


def kernel(count, dens_hbm, near_hbm, neigh_hbm, live_hbm, cmap_hbm, rest_hbm, eval_hbm, coup_hbm, out, neigh, live,
           cmap, coup, low, high, near, rest, evl, moments, local_exp, acc, in_sem, near_sem, halo_send, halo_recv, own_send, own_recv, relay_send, relay_recv):
    slots, blk_count = neigh.shape
    reach = blk_count // 2
    columns = low.shape[1]
    coarse_dev = moments.shape[1]
    zero_slot = low.shape[0] - 1
    chips = count // 2
    chunks = blk_count // CHUNK
    me = lax.axis_index("panel")
    core = lax.rem(me, 2)
    chip = me // 2
    partner = me + 1 - 2 * core

    dens_copy = pltpu.make_async_copy(dens_hbm, low.at[pl.ds(reach, blk_count)], in_sem.at[0])
    high_copy = pltpu.make_async_copy(dens_hbm, high.at[pl.ds(0, blk_count)], in_sem.at[7])
    rest_copy = pltpu.make_async_copy(rest_hbm, rest, in_sem.at[1])
    eval_copy = pltpu.make_async_copy(eval_hbm, evl, in_sem.at[2])
    cmap_copy = pltpu.make_async_copy(cmap_hbm, cmap, in_sem.at[3])
    neigh_copy = pltpu.make_async_copy(neigh_hbm, neigh, in_sem.at[4])
    live_copy = pltpu.make_async_copy(live_hbm, live, in_sem.at[5])
    coup_copy = pltpu.make_async_copy(coup_hbm, coup, in_sem.at[6])

    def near_copy(i):
        part = pl.ds(i * CHUNK, CHUNK)
        return pltpu.make_async_copy(near_hbm.at[part], near.at[part], near_sem.at[i])

    dens_copy.start()
    high_copy.start()
    rest_copy.start()
    for copy in (cmap_copy, neigh_copy, live_copy, coup_copy):
        copy.start()

    barrier = pltpu.get_barrier_semaphore()
    has_low = me > 0
    has_high = me < count - 1
    for d in range(1, chips):
        pl.semaphore_signal(barrier, inc=1, device_id={"panel": lax.rem(chip + d, chips) * 2 + core})
    pl.semaphore_signal(barrier, inc=1, device_id={"panel": partner})

    beside = lax.rem(me + 2 * core - 1 + count, count)
    pl.semaphore_signal(barrier, inc=1, device_id={"panel": beside})

    low[zero_slot] = jnp.zeros(low.shape[1:], low.dtype)
    high[zero_slot] = jnp.zeros(high.shape[1:], high.dtype)

    @pl.when(me == 0)
    def _():
        low[pl.ds(0, reach)] = jnp.zeros((reach,) + low.shape[1:], low.dtype)

    @pl.when(me == count - 1)
    def _():
        high[pl.ds(blk_count, reach)] = jnp.zeros((reach,) + high.shape[1:], high.dtype)

    dens_copy.wait()
    cmap_copy.wait()
    rest_copy.wait()
    first = (1 - core) * (chunks // 2)
    for i in range(chunks):
        near_copy(lax.rem(first + i, chunks)).start()
    eval_copy.start()
    total = jnp.zeros((coarse_dev * columns, rest.shape[1]), jnp.float32)
    step = 8
    for b0 in range(0, blk_count, step):
        rows = []
        for b in range(b0, b0 + step):
            own = cmap[b] - me * coarse_dev
            values = low[reach + b].astype(jnp.float32)
            masked = [values * (own == c).astype(jnp.float32) for c in range(coarse_dev)]
            rows.append(jnp.concatenate(masked, axis=0).astype(jnp.bfloat16))
        weights = jnp.concatenate([rest[b] for b in range(b0, b0 + step)], axis=1)
        total += lax.dot_general(jnp.concatenate(rows, axis=1), weights, CONTRACT_LAST,
                                 preferred_element_type=jnp.float32)
    moments[me] = total.reshape(moments.shape[1:]).astype(jnp.bfloat16)

    pl.semaphore_wait(barrier, chips + 1)

    def halo(up):
        return pltpu.make_async_remote_copy(
            src_ref=low.at[pl.ds(blk_count if up else reach, reach)],
            dst_ref=low.at[pl.ds(0, reach)] if up else high.at[pl.ds(blk_count, reach)],
            send_sem=halo_send.at[int(up)], recv_sem=halo_recv.at[int(up)],
            device_id={"panel": me + 1 if up else me - 1})

    def own_copy(d):
        return pltpu.make_async_remote_copy(
            src_ref=moments.at[me], dst_ref=moments.at[me], send_sem=own_send.at[d], recv_sem=own_recv.at[d],
            device_id={"panel": lax.rem(chip + d, chips) * 2 + core if d else partner})

    def own_arrival(d):
        source = lax.rem(chip + chips - d, chips) * 2 + core if d else partner
        return pltpu.make_async_remote_copy(
            src_ref=moments.at[source], dst_ref=moments.at[source], send_sem=own_send.at[d], recv_sem=own_recv.at[d],
            device_id={"panel": source})

    def relay_copy(d):
        source = lax.rem(chip + chips - d, chips) * 2 + core
        return pltpu.make_async_remote_copy(
            src_ref=moments.at[source], dst_ref=moments.at[source], send_sem=relay_send.at[d],
            recv_sem=relay_recv.at[d], device_id={"panel": partner})

    def relay_arrival(d):
        source = lax.rem(chip + chips - d, chips) * 2 + 1 - core
        return pltpu.make_async_remote_copy(
            src_ref=moments.at[source], dst_ref=moments.at[source], send_sem=relay_send.at[d],
            recv_sem=relay_recv.at[d], device_id={"panel": partner})

    @pl.when(has_high)
    def _():
        halo(True).start()

    @pl.when(has_low)
    def _():
        halo(False).start()

    for d in range(chips):
        own_copy(d).start()

    neigh_copy.wait()
    live_copy.wait()
    high_copy.wait()

    def near_half(field, first, base):
        def near_step(i, carry):
            near_copy(first + i).wait()
            for t in range(CHUNK):
                b = (first + i) * CHUNK + t
                alive = live[b]
                places = [jnp.clip(neigh[j, b] - base, 0, zero_slot - 1) for j in range(slots)]
                picked = [field[jnp.where(j < alive, places[j], zero_slot)] for j in range(slots)]
                weights = jnp.concatenate([near[b, j] for j in range(slots)], axis=1)
                acc[b] = lax.dot_general(jnp.concatenate(picked, axis=1), weights, CONTRACT_LAST,
                                         preferred_element_type=jnp.float32)
            return carry

        lax.fori_loop(0, half, near_step, 0)

    half = chunks // 2
    low_half = functools.partial(near_half, low, 0, me * blk_count - reach)
    high_half = functools.partial(near_half, high, half, me * blk_count)

    @pl.when(core == 1)
    def _():
        halo(True).wait_recv()
        low_half()

    @pl.when(core == 0)
    def _():
        halo(False).wait_recv()
        high_half()

    for d in range(1, chips):
        own_arrival(d).wait_recv()
        relay_copy(d).start()

    @pl.when((core == 0) & has_low)
    def _():
        halo(True).wait_recv()

    @pl.when((core == 1) & has_high)
    def _():
        halo(False).wait_recv()

    @pl.when(core == 0)
    def _():
        low_half()

    @pl.when(core == 1)
    def _():
        high_half()

    coup_copy.wait()
    own_arrival(0).wait_recv()
    for d in range(1, chips):
        relay_arrival(d).wait_recv()

    sums = [jnp.zeros(moments.shape[2:], jnp.float32) for _ in range(coarse_dev)]
    for s in range(count):
        for i in range(coarse_dev):
            term = moments[s, i].astype(jnp.float32)
            for c in range(coarse_dev):
                sums[c] += coup[c, s * coarse_dev + i] * term
    for c in range(coarse_dev):
        local_exp[c] = sums[c].astype(jnp.bfloat16)

    eval_copy.wait()

    for b in range(blk_count):
        spread = local_exp[jnp.clip(cmap[b] - me * coarse_dev, 0, coarse_dev - 1)]
        far = jnp.dot(spread, evl[b], preferred_element_type=jnp.float32)
        out[b] = (acc[b] + far).astype(jnp.bfloat16)

    @pl.when(has_high)
    def _():
        halo(True).wait_send()

    @pl.when(has_low)
    def _():
        halo(False).wait_send()

    own_copy(0).wait_send()
    for d in range(1, chips):
        own_copy(d).wait_send()
        relay_copy(d).wait_send()


def shards(count, density, near_blocks, neighbours, counts, coarse_map, restrict, evaluate, coupling):
    blk_count, columns, panels = density.shape
    terms = restrict.shape[1]
    coarse_dev = coupling.shape[0]
    chips = count // 2
    hbm = pl.BlockSpec(memory_space=pl.ANY)
    return pl.pallas_call(
        functools.partial(kernel, count),
        out_shape=pltpu.VMEM(density.shape, jnp.bfloat16),
        in_specs=[hbm] * 8,
        out_specs=pl.BlockSpec(memory_space=pltpu.VMEM),
        scratch_shapes=[
            pltpu.SMEM(neighbours.shape[::-1], jnp.int32),
            pltpu.SMEM(counts.shape, jnp.int32),
            pltpu.SMEM(coarse_map.shape, jnp.int32),
            pltpu.SMEM(coupling.shape, jnp.float32),
            pltpu.VMEM((blk_count + blk_count // 2 + 1, columns, panels), jnp.bfloat16),
            pltpu.VMEM((blk_count + blk_count // 2 + 1, columns, panels), jnp.bfloat16),
            pltpu.VMEM(near_blocks.shape, jnp.bfloat16),
            pltpu.VMEM(restrict.shape, jnp.bfloat16),
            pltpu.VMEM(evaluate.shape, jnp.bfloat16),
            pltpu.VMEM((count, coarse_dev, columns, terms), jnp.bfloat16),
            pltpu.VMEM((coarse_dev, columns, terms), jnp.bfloat16),
            pltpu.VMEM(density.shape, jnp.float32),
            pltpu.SemaphoreType.DMA((8,)),
            pltpu.SemaphoreType.DMA((blk_count // CHUNK,)),
            pltpu.SemaphoreType.DMA((2,)),
            pltpu.SemaphoreType.DMA((2,)),
            pltpu.SemaphoreType.DMA((chips,)),
            pltpu.SemaphoreType.DMA((chips,)),
            pltpu.SemaphoreType.DMA((chips,)),
            pltpu.SemaphoreType.DMA((chips,)),
        ],
        compiler_params=pltpu.CompilerParams(collective_id=0, has_side_effects=True),
    )(density, near_blocks, neighbours.T, counts, coarse_map, restrict, evaluate, coupling)


def solution(mesh):
    rows = ("grp", "panel")
    placed = (
        P(rows, None, None),
        P(rows, None, None, None),
        P(rows, None),
        P(rows),
        P(rows),
        P(rows, None, None),
        P(rows, None, None),
        P(rows, None),
    )
    return jax.shard_map(
        functools.partial(shards, mesh.shape["panel"]),
        mesh=mesh,
        in_specs=placed,
        out_specs=P(rows, None, None),
        check_vma=False,
    )
```

profile of v0, /device:TPU:0, one launch (start us, length us, event | category | flops | bytes accessed | tf_op | source)
XLA Modules:
  0.0 12.4 jit_solution(17898019484459939531)
XLA Ops:
  0.0 11.8 %shard_map.82 = bf16[32,16,128]{2,1,0:T(8,128)(2,1)S(1)} custom-call(bf16[32,16,128]{2,1,0:T(8,128)(2,1)} %dens_hbm.1, bf16[32,8,128,128]{3,2,1,0:T(8,128)(2,1)} %near_hbm.1, s32[8,32]{1,0:T(8,128)} %bitcast.1, s32[32]{0:T(128)} %live_hbm.1, s32[32]{0:T(128)} %cmap_hbm.1, bf16[32,128,128]{2,1,0:T(8,128)(2,1)} %rest_hbm.1, bf16[32,128,128]{2,1,0:T(8,128)(2,1)} %eval_hbm.1, ...), custom_call_target="tpu_custom_call" | custom-call | tf_op jit(solution)/shard_map/pallas_call | solution.py:226
  11.8 0.7 %copy.10 = bf16[32,16,128]{2,1,0:T(8,128)(2,1)} copy(bf16[32,16,128]{2,1,0:T(8,128)(2,1)S(1)} %shard_map.82) | data formatting | bytes 262144
where the time goes:
time: 12.6 us; the launch traced here: 12.4 us
  Pallas kernels  11.8 us (94%)
  local copies, waits for them, and re-layouts  0.66 us (5%)
    pallas_call x1, Pallas kernels, shards(): pl.pallas_call(functools.partial(kernel, count), out_shape=pltpu.VMEM(den...  11.8 us
    unnamed x1, local copies, waits for them, and re-layouts  0.66 us

commit v1 on v0

v1 whole, which is shorter than its diff:
```python
import functools

import jax
import jax.numpy as jnp
from jax import lax
from jax.experimental import pallas as pl
from jax.experimental.pallas import tpu as pltpu
from jax.sharding import PartitionSpec as P

PARTS = 4
CONTRACT_LAST = (((1,), (1,)), ((), ()))


def kernel(count, dens_hbm, near_hbm, neigh_hbm, live_hbm, cmap_hbm, rest_hbm, eval_hbm, coup_hbm, out, neigh, live,
           cmap, coup, low, high, near, rest, evl, masked, moments, local_exp, acc, in_sem, rest_sem, near_sem, halo_send,
           halo_recv, send_sem, early_recv, late_recv, next_ready, ready, last_ready):
    slots, blk_count = neigh.shape
    reach = blk_count // 2
    columns = low.shape[1]
    coarse_dev = moments.shape[1]
    zero_slot = low.shape[0] - 1
    chips = count // 2
    last = chips - 1
    part = blk_count // PARTS
    me = lax.axis_index("panel")
    core = lax.rem(me, 2)
    chip = me // 2
    has_low = me > 0
    has_high = me < count - 1

    dens_copy = pltpu.make_async_copy(dens_hbm, low.at[pl.ds(reach, blk_count)], in_sem.at[0])
    high_copy = pltpu.make_async_copy(dens_hbm, high.at[pl.ds(0, blk_count)], in_sem.at[6])
    cmap_copy = pltpu.make_async_copy(cmap_hbm, cmap, in_sem.at[1])
    neigh_copy = pltpu.make_async_copy(neigh_hbm, neigh, in_sem.at[2])
    live_copy = pltpu.make_async_copy(live_hbm, live, in_sem.at[3])
    coup_copy = pltpu.make_async_copy(coup_hbm, coup, in_sem.at[4])
    eval_copy = pltpu.make_async_copy(eval_hbm, evl, in_sem.at[5])

    def rest_copy(i):
        blocks = pl.ds(i * part, part)
        return pltpu.make_async_copy(rest_hbm.at[blocks], rest.at[blocks], rest_sem.at[i])

    def near_copy(i):
        blocks = pl.ds(i * part, part)
        return pltpu.make_async_copy(near_hbm.at[blocks], near.at[blocks], near_sem.at[i])

    dens_copy.start()
    cmap_copy.start()
    for i in range(PARTS):
        rest_copy(i).start()
    high_copy.start()
    neigh_copy.start()
    live_copy.start()
    coup_copy.start()

    barrier = pltpu.get_barrier_semaphore()

    def greet(t, carry):
        pl.semaphore_signal(barrier, inc=1, device_id={"panel": t})
        return carry

    def answer(t, carry):
        pl.semaphore_signal(ready, inc=1, device_id={"panel": t})
        return carry

    def answer_last(t, carry):
        pl.semaphore_signal(last_ready, inc=1, device_id={"panel": t})
        return carry

    lax.fori_loop(me + 1, count, greet, 0)
    low[zero_slot] = jnp.zeros(low.shape[1:], low.dtype)
    high[zero_slot] = jnp.zeros(high.shape[1:], high.dtype)

    @pl.when(me == 0)
    def _():
        low[pl.ds(0, reach)] = jnp.zeros((reach,) + low.shape[1:], low.dtype)

    @pl.when(me == count - 1)
    def _():
        high[pl.ds(blk_count, reach)] = jnp.zeros((reach,) + high.shape[1:], high.dtype)

    @pl.when(has_low)
    def _():
        pl.semaphore_wait(barrier, me)
        pl.semaphore_signal(next_ready, inc=1, device_id={"panel": me - 1})

    @pl.when(chip < last)
    def _():
        lax.fori_loop(0, me, answer, 0)

    @pl.when(chip == last)
    def _():
        lax.fori_loop(0, me, answer_last, 0)

    dens_copy.wait()
    cmap_copy.wait()
    for b in range(blk_count):
        own = cmap[b] - me * coarse_dev
        values = low[reach + b].astype(jnp.float32)
        rows = [values * (own == c).astype(jnp.float32) for c in range(coarse_dev)]
        masked[b] = jnp.concatenate(rows, axis=0).astype(jnp.bfloat16)

    def halo(up):
        return pltpu.make_async_remote_copy(
            src_ref=low.at[pl.ds(blk_count if up else reach, reach)],
            dst_ref=low.at[pl.ds(0, reach)] if up else high.at[pl.ds(blk_count, reach)],
            send_sem=halo_send.at[int(up)], recv_sem=halo_recv.at[int(up)],
            device_id={"panel": me + 1 if up else me - 1})

    @pl.when(has_low & (chip < last))
    def _():
        halo(False).start()

    total = jnp.zeros((coarse_dev * columns, rest.shape[1]), jnp.float32)
    for i in range(PARTS):
        rest_copy(i).wait()
        if i == PARTS - 1:
            for k in range(PARTS):
                near_copy(lax.rem(k + (1 - core) * (PARTS // 2), PARTS)).start()
            eval_copy.start()
        blocks = range(i * part, (i + 1) * part)
        values = jnp.concatenate([masked[b] for b in blocks], axis=1)
        weights = jnp.concatenate([rest[b] for b in blocks], axis=1)
        total += lax.dot_general(values, weights, CONTRACT_LAST, preferred_element_type=jnp.float32)
    moments[me] = total.reshape(moments.shape[1:]).astype(jnp.bfloat16)

    def moment_copy(target, recv_sem):
        return pltpu.make_async_remote_copy(
            src_ref=moments.at[me], dst_ref=moments.at[me], send_sem=send_sem, recv_sem=recv_sem,
            device_id={"panel": target})

    def send(t, carry):
        moment_copy(t, early_recv).start()
        return carry

    def send_late(t, carry):
        moment_copy(t, late_recv).start()
        return carry

    @pl.when(chip < last)
    def _():
        lax.fori_loop(0, me, send, 0)

    @pl.when(chip == last)
    def _():
        lax.fori_loop(0, me, send_late, 0)

    @pl.when(chip == last)
    def _():
        halo(False).start()

    @pl.when(has_high)
    def _():
        pl.semaphore_wait(next_ready, 1)
        halo(True).start()

    @pl.when(me < count - 3)
    def _():
        pl.semaphore_wait(ready, count - 3 - me)
        lax.fori_loop(me + 1, count - 2, send, 0)

    @pl.when(chip < last)
    def _():
        pl.semaphore_wait(last_ready, 2)
        lax.fori_loop(count - 2, count, send, 0)

    @pl.when(me == count - 2)
    def _():
        pl.semaphore_wait(last_ready, 1)
        send_late(count - 1, 0)

    neigh_copy.wait()
    live_copy.wait()
    high_copy.wait()
    half = PARTS // 2

    def near_half(field, first, base):
        def near_part(i, carry):
            near_copy(first + i).wait()
            for t in range(part):
                b = (first + i) * part + t
                alive = live[b]
                places = [jnp.clip(neigh[j, b] - base, 0, zero_slot - 1) for j in range(slots)]
                picked = [field[jnp.where(j < alive, places[j], zero_slot)] for j in range(slots)]
                weights = jnp.concatenate([near[b, j] for j in range(slots)], axis=1)
                acc[b] = lax.dot_general(jnp.concatenate(picked, axis=1), weights, CONTRACT_LAST,
                                         preferred_element_type=jnp.float32)
            return carry

        lax.fori_loop(0, half, near_part, 0)

    def low_half():
        @pl.when(has_low)
        def _():
            halo(True).wait_recv()

        near_half(low, 0, me * blk_count - reach)

    def high_half():
        @pl.when(has_high)
        def _():
            halo(False).wait_recv()

        near_half(high, half, me * blk_count)

    @pl.when(core == 1)
    def _():
        low_half()
        high_half()

    @pl.when(core == 0)
    def _():
        high_half()
        low_half()

    def bytes_of(n, sem):
        block = moments.at[pl.ds(0, n)]
        return pltpu.make_async_copy(block, block, sem)

    coup_copy.wait()
    eval_copy.wait()

    @pl.when(chip < last)
    def _():
        bytes_of(count - 3, early_recv).wait()

    @pl.when(chip == last)
    def _():
        bytes_of(count - 2, early_recv).wait()

    sums = [jnp.zeros(moments.shape[2:], jnp.float32) for _ in range(coarse_dev)]

    def add(s):
        for i in range(coarse_dev):
            term = moments[s, i].astype(jnp.float32)
            for c in range(coarse_dev):
                sums[c] += coup[c, s * coarse_dev + i] * term

    for s in range(count - 2):
        add(s)

    @pl.when(chip < last)
    def _():
        bytes_of(2, late_recv).wait()

    @pl.when(chip == last)
    def _():
        bytes_of(1, late_recv).wait()

    add(count - 2)
    add(count - 1)
    for c in range(coarse_dev):
        local_exp[c] = sums[c].astype(jnp.bfloat16)

    for b in range(blk_count):
        spread = local_exp[jnp.clip(cmap[b] - me * coarse_dev, 0, coarse_dev - 1)]
        far = jnp.dot(spread, evl[b], preferred_element_type=jnp.float32)
        out[b] = (acc[b] + far).astype(jnp.bfloat16)

    @pl.when(has_high)
    def _():
        halo(True).wait_send()

    @pl.when(has_low)
    def _():
        halo(False).wait_send()

    bytes_of(count - 1, send_sem).wait()


def shards(count, density, near_blocks, neighbours, counts, coarse_map, restrict, evaluate, coupling):
    blk_count, columns, panels = density.shape
    terms = restrict.shape[1]
    coarse_dev = coupling.shape[0]
    hbm = pl.BlockSpec(memory_space=pl.ANY)
    dma = pltpu.SemaphoreType.DMA
    return pl.pallas_call(
        functools.partial(kernel, count),
        out_shape=pltpu.VMEM(density.shape, jnp.bfloat16),
        in_specs=[hbm] * 8,
        out_specs=pl.BlockSpec(memory_space=pltpu.VMEM),
        scratch_shapes=[
            pltpu.SMEM(neighbours.shape[::-1], jnp.int32),
            pltpu.SMEM(counts.shape, jnp.int32),
            pltpu.SMEM(coarse_map.shape, jnp.int32),
            pltpu.SMEM(coupling.shape, jnp.float32),
            pltpu.VMEM((blk_count + blk_count // 2 + 1, columns, panels), jnp.bfloat16),
            pltpu.VMEM((blk_count + blk_count // 2 + 1, columns, panels), jnp.bfloat16),
            pltpu.VMEM(near_blocks.shape, jnp.bfloat16),
            pltpu.VMEM(restrict.shape, jnp.bfloat16),
            pltpu.VMEM(evaluate.shape, jnp.bfloat16),
            pltpu.VMEM((blk_count, coarse_dev * columns, panels), jnp.bfloat16),
            pltpu.VMEM((count, coarse_dev, columns, terms), jnp.bfloat16),
            pltpu.VMEM((coarse_dev, columns, terms), jnp.bfloat16),
            pltpu.VMEM(density.shape, jnp.float32),
            dma((7,)),
            dma((PARTS,)),
            dma((PARTS,)),
            dma((2,)),
            dma((2,)),
            dma,
            dma,
            dma,
            pltpu.SemaphoreType.REGULAR,
            pltpu.SemaphoreType.REGULAR,
            pltpu.SemaphoreType.REGULAR,
        ],
        compiler_params=pltpu.CompilerParams(collective_id=0, has_side_effects=True),
    )(density, near_blocks, neighbours.T, counts, coarse_map, restrict, evaluate, coupling)


def solution(mesh):
    rows = ("grp", "panel")
    placed = (
        P(rows, None, None),
        P(rows, None, None, None),
        P(rows, None),
        P(rows),
        P(rows),
        P(rows, None, None),
        P(rows, None, None),
        P(rows, None),
    )
    return jax.shard_map(
        functools.partial(shards, mesh.shape["panel"]),
        mesh=mesh,
        in_specs=placed,
        out_specs=P(rows, None, None),
        check_vma=False,
    )
```

time: 12.6 us -> 11.1 us (0.88)
  Pallas kernels: 11.8 us -> 10.3 us
    pallas_call x1, Pallas kernels: 11.8 us -> 10.3 us  [shards(): pl.pallas_call(functools.partial(kernel, count), out_shape=pltpu.VMEM(den...]
where the time goes in v1:
time: 11.1 us; the launch traced here: 11 us
  Pallas kernels  10.3 us (93%)
  local copies, waits for them, and re-layouts  0.66 us (6%)
    pallas_call x1, Pallas kernels, shards(): pl.pallas_call(functools.partial(kernel, count), out_shape=pltpu.VMEM(den...  10.3 us
    unnamed x1, local copies, waits for them, and re-layouts  0.66 us

profile of v1, /device:TPU:0, one launch (start us, length us, event | category | flops | bytes accessed | tf_op | source)
XLA Modules:
  0.0 11.0 jit_solution(17088827853327542480)
XLA Ops:
  0.0 10.3 %shard_map.82 = bf16[32,16,128]{2,1,0:T(8,128)(2,1)S(1)} custom-call(bf16[32,16,128]{2,1,0:T(8,128)(2,1)} %dens_hbm.1, bf16[32,8,128,128]{3,2,1,0:T(8,128)(2,1)} %near_hbm.1, s32[8,32]{1,0:T(8,128)} %bitcast.1, s32[32]{0:T(128)} %live_hbm.1, s32[32]{0:T(128)} %cmap_hbm.1, bf16[32,128,128]{2,1,0:T(8,128)(2,1)} %rest_hbm.1, bf16[32,128,128]{2,1,0:T(8,128)(2,1)} %eval_hbm.1, ...), custom_call_target="tpu_custom_call" | custom-call | tf_op jit(solution)/shard_map/pallas_call | solution.py:277
  10.3 0.7 %copy.10 = bf16[32,16,128]{2,1,0:T(8,128)(2,1)} copy(bf16[32,16,128]{2,1,0:T(8,128)(2,1)S(1)} %shard_map.82) | data formatting | bytes 262144

commit v2 on v1

v2 whole, which is shorter than its diff:
```python
import functools

import jax
import jax.numpy as jnp
from jax import lax
from jax.experimental import pallas as pl
from jax.experimental.pallas import tpu as pltpu
from jax.sharding import PartitionSpec as P

PARTS = 4
CONTRACT_LAST = (((1,), (1,)), ((), ()))


def kernel(count, dens_hbm, near_hbm, neigh_hbm, live_hbm, cmap_hbm, rest_hbm, eval_hbm, coup_hbm, out, neigh, live,
           cmap, coup, low, high, near, rest, evl, masked, moments, acc, halo_recv, early_recv, late_recv, next_ready, ready, last_ready):
    slots, blk_count = neigh.shape
    reach = blk_count // 2
    columns, panels = low.shape[1:]
    coarse_dev = moments.shape[1]
    zero_slot = low.shape[0] - 1
    chips = count // 2
    last = chips - 1
    part = blk_count // PARTS
    me = lax.axis_index("panel")
    core = lax.rem(me, 2)
    chip = me // 2
    has_low = me > 0
    has_high = me < count - 1

    def bytes_of(n, sem):
        block = moments.at[pl.ds(0, n)]
        return pltpu.make_async_copy(block, block, sem)

    def gather(in_sem, rest_sem, near_sem, halo_send, send_sem):
        dens_copy = pltpu.make_async_copy(dens_hbm, low.at[pl.ds(reach, blk_count)], in_sem.at[0])
        high_copy = pltpu.make_async_copy(dens_hbm, high.at[pl.ds(0, blk_count)], in_sem.at[6])
        cmap_copy = pltpu.make_async_copy(cmap_hbm, cmap, in_sem.at[1])
        neigh_copy = pltpu.make_async_copy(neigh_hbm, neigh, in_sem.at[2])
        live_copy = pltpu.make_async_copy(live_hbm, live, in_sem.at[3])
        coup_copy = pltpu.make_async_copy(coup_hbm, coup, in_sem.at[4])
        eval_copy = pltpu.make_async_copy(eval_hbm, evl, in_sem.at[5])

        def rest_copy(i):
            blocks = pl.ds(i * part, part)
            return pltpu.make_async_copy(rest_hbm.at[blocks], rest.at[blocks], rest_sem.at[i])

        def near_copy(i):
            blocks = pl.ds(i * part, part)
            return pltpu.make_async_copy(near_hbm.at[blocks], near.at[blocks], near_sem.at[i])

        dens_copy.start()
        cmap_copy.start()
        for i in range(PARTS):
            rest_copy(i).start()
        high_copy.start()
        neigh_copy.start()
        live_copy.start()
        coup_copy.start()

        barrier = pltpu.get_barrier_semaphore()

        def greet(t, carry):
            pl.semaphore_signal(barrier, inc=1, device_id={"panel": t})
            return carry

        def answer(t, carry):
            pl.semaphore_signal(ready, inc=1, device_id={"panel": t})
            return carry

        def answer_last(t, carry):
            pl.semaphore_signal(last_ready, inc=1, device_id={"panel": t})
            return carry

        lax.fori_loop(me + 1, count, greet, 0)
        low[zero_slot] = jnp.zeros(low.shape[1:], low.dtype)
        high[zero_slot] = jnp.zeros(high.shape[1:], high.dtype)

        @pl.when(me == 0)
        def _():
            low[pl.ds(0, reach)] = jnp.zeros((reach,) + low.shape[1:], low.dtype)

        @pl.when(me == count - 1)
        def _():
            high[pl.ds(blk_count, reach)] = jnp.zeros((reach,) + high.shape[1:], high.dtype)

        @pl.when(has_low)
        def _():
            pl.semaphore_wait(barrier, me)
            pl.semaphore_signal(next_ready, inc=1, device_id={"panel": me - 1})

        @pl.when(chip < last)
        def _():
            lax.fori_loop(0, me, answer, 0)

        @pl.when(chip == last)
        def _():
            lax.fori_loop(0, me, answer_last, 0)

        dens_copy.wait()
        cmap_copy.wait()
        for b in range(blk_count):
            own = cmap[b] - me * coarse_dev
            values = low[reach + b].astype(jnp.float32)
            rows = [values * (own == c).astype(jnp.float32) for c in range(coarse_dev)]
            masked[b] = jnp.concatenate(rows, axis=0).astype(jnp.bfloat16)

        def halo(up):
            return pltpu.make_async_remote_copy(
                src_ref=low.at[pl.ds(blk_count if up else reach, reach)],
                dst_ref=low.at[pl.ds(0, reach)] if up else high.at[pl.ds(blk_count, reach)],
                send_sem=halo_send.at[int(up)], recv_sem=halo_recv.at[int(up)],
                device_id={"panel": me + 1 if up else me - 1})

        @pl.when(has_low & (chip < last - 1))
        def _():
            halo(False).start()

        total = jnp.zeros((coarse_dev * columns, rest.shape[1]), jnp.float32)
        for i in range(PARTS):
            rest_copy(i).wait()
            blocks = range(i * part, (i + 1) * part)
            values = jnp.concatenate([masked[b] for b in blocks], axis=1)
            weights = jnp.concatenate([rest[b] for b in blocks], axis=1)
            total += lax.dot_general(values, weights, CONTRACT_LAST, preferred_element_type=jnp.float32)
        moments[me] = total.reshape(moments.shape[1:]).astype(jnp.bfloat16)

        def moment_copy(target, recv_sem):
            return pltpu.make_async_remote_copy(
                src_ref=moments.at[me], dst_ref=moments.at[me], send_sem=send_sem, recv_sem=recv_sem,
                device_id={"panel": target})

        def send(t, carry):
            moment_copy(t, early_recv).start()
            return carry

        def send_late(t, carry):
            moment_copy(t, late_recv).start()
            return carry

        @pl.when(chip < last)
        def _():
            lax.fori_loop(0, me, send, 0)

        @pl.when(chip == last)
        def _():
            lax.fori_loop(0, me, send_late, 0)

        @pl.when(chip >= last - 1)
        def _():
            halo(False).start()

        for k in range(PARTS):
            near_copy(lax.rem(k + (1 - core) * (PARTS // 2), PARTS)).start()
        eval_copy.start()

        @pl.when(has_high)
        def _():
            pl.semaphore_wait(next_ready, 1)
            halo(True).start()

        @pl.when(me < count - 3)
        def _():
            pl.semaphore_wait(ready, count - 3 - me)
            lax.fori_loop(me + 1, count - 2, send, 0)

        @pl.when(chip < last)
        def _():
            pl.semaphore_wait(last_ready, 2)
            lax.fori_loop(count - 2, count, send, 0)

        @pl.when(me == count - 2)
        def _():
            pl.semaphore_wait(last_ready, 1)
            send_late(count - 1, 0)

        neigh_copy.wait()
        live_copy.wait()
        high_copy.wait()
        half = PARTS // 2

        def near_half(field, first, base):
            def near_part(i, carry):
                near_copy(first + i).wait()
                for t in range(part):
                    b = (first + i) * part + t
                    alive = live[b]
                    places = [jnp.clip(neigh[j, b] - base, 0, zero_slot - 1) for j in range(slots)]
                    picked = [field[jnp.where(j < alive, places[j], zero_slot)] for j in range(slots)]
                    weights = jnp.concatenate([near[b, j] for j in range(slots)], axis=1)
                    acc[b] = lax.dot_general(jnp.concatenate(picked, axis=1), weights, CONTRACT_LAST,
                                             preferred_element_type=jnp.float32)
                return carry

            lax.fori_loop(0, half, near_part, 0)

        def low_half():
            @pl.when(has_low)
            def _():
                halo(True).wait_recv()

            near_half(low, 0, me * blk_count - reach)

        def high_half():
            @pl.when(has_high)
            def _():
                halo(False).wait_recv()

            near_half(high, half, me * blk_count)

        @pl.when(core == 1)
        def _():
            low_half()
            high_half()

        @pl.when(core == 0)
        def _():
            high_half()
            low_half()

        coup_copy.wait()
        eval_copy.wait()

        @pl.when(has_high)
        def _():
            halo(True).wait_send()

        @pl.when(has_low)
        def _():
            halo(False).wait_send()

        bytes_of(count - 1, send_sem).wait()

    dma = pltpu.SemaphoreType.DMA
    pl.run_scoped(gather, dma((7,)), dma((PARTS,)), dma((PARTS,)), dma((2,)), dma)

    @pl.when(chip < last)
    def _():
        bytes_of(count - 3, early_recv).wait()

    @pl.when(chip == last)
    def _():
        bytes_of(count - 2, early_recv).wait()

    sums = [jnp.zeros(moments.shape[2:], jnp.float32) for _ in range(coarse_dev)]

    def add(s):
        for i in range(coarse_dev):
            term = moments[s, i].astype(jnp.float32)
            for c in range(coarse_dev):
                sums[c] += coup[c, s * coarse_dev + i] * term

    for s in range(count - 2):
        add(s)

    @pl.when(chip < last)
    def _():
        bytes_of(2, late_recv).wait()

    @pl.when(chip == last)
    def _():
        bytes_of(1, late_recv).wait()

    add(count - 2)
    add(count - 1)
    spread = [total.astype(jnp.bfloat16) for total in sums]
    blank = jnp.zeros_like(spread[0])
    lhs = jnp.concatenate([jnp.concatenate([e, blank], axis=1) for e in spread]
                          + [jnp.concatenate([blank, e], axis=1) for e in spread], axis=0)
    for b0 in range(0, blk_count, 4):
        rhs = jnp.concatenate([jnp.concatenate([evl[b0 + i], evl[b0 + i + 1]], axis=1) for i in (0, 2)], axis=0)
        far = jnp.dot(lhs, rhs, preferred_element_type=jnp.float32)
        for i in range(4):
            b = b0 + i
            own = cmap[b] - me * coarse_dev
            lanes = slice((i % 2) * panels, (i % 2 + 1) * panels)
            first = (i // 2) * coarse_dev * columns
            part_far = far[first:first + columns, lanes]
            for c in range(1, coarse_dev):
                rows = first + c * columns
                part_far = jnp.where(own == c, far[rows:rows + columns, lanes], part_far)
            out[b] = (acc[b] + part_far).astype(jnp.bfloat16)


def shards(count, density, near_blocks, neighbours, counts, coarse_map, restrict, evaluate, coupling):
    blk_count, columns, panels = density.shape
    terms = restrict.shape[1]
    coarse_dev = coupling.shape[0]
    hbm = pl.BlockSpec(memory_space=pl.ANY)
    dma = pltpu.SemaphoreType.DMA
    return pl.pallas_call(
        functools.partial(kernel, count),
        out_shape=pltpu.VMEM(density.shape, jnp.bfloat16),
        in_specs=[hbm] * 8,
        out_specs=pl.BlockSpec(memory_space=pltpu.VMEM),
        scratch_shapes=[
            pltpu.SMEM(neighbours.shape[::-1], jnp.int32),
            pltpu.SMEM(counts.shape, jnp.int32),
            pltpu.SMEM(coarse_map.shape, jnp.int32),
            pltpu.SMEM(coupling.shape, jnp.float32),
            pltpu.VMEM((blk_count + blk_count // 2 + 1, columns, panels), jnp.bfloat16),
            pltpu.VMEM((blk_count + blk_count // 2 + 1, columns, panels), jnp.bfloat16),
            pltpu.VMEM(near_blocks.shape, jnp.bfloat16),
            pltpu.VMEM(restrict.shape, jnp.bfloat16),
            pltpu.VMEM(evaluate.shape, jnp.bfloat16),
            pltpu.VMEM((blk_count, coarse_dev * columns, panels), jnp.bfloat16),
            pltpu.VMEM((count, coarse_dev, columns, terms), jnp.bfloat16),
            pltpu.VMEM(density.shape, jnp.float32),
            dma((2,)),
            dma,
            dma,
            pltpu.SemaphoreType.REGULAR,
            pltpu.SemaphoreType.REGULAR,
            pltpu.SemaphoreType.REGULAR,
        ],
        compiler_params=pltpu.CompilerParams(collective_id=0, has_side_effects=True),
    )(density, near_blocks, neighbours.T, counts, coarse_map, restrict, evaluate, coupling)


def solution(mesh):
    rows = ("grp", "panel")
    placed = (
        P(rows, None, None),
        P(rows, None, None, None),
        P(rows, None),
        P(rows),
        P(rows),
        P(rows, None, None),
        P(rows, None, None),
        P(rows, None),
    )
    return jax.shard_map(
        functools.partial(shards, mesh.shape["panel"]),
        mesh=mesh,
        in_specs=placed,
        out_specs=P(rows, None, None),
        check_vma=False,
    )
```

time: 11.1 us -> 10.9 us (0.982)
  Pallas kernels: 10.3 us -> 10.1 us
    pallas_call x1, Pallas kernels: 10.3 us -> 10.1 us  [shards(): pl.pallas_call(functools.partial(kernel, count), out_shape=pltpu.VMEM(den...]
where the time goes in v2:
time: 10.9 us; the launch traced here: 10.7 us
  Pallas kernels  10.1 us (93%)
  local copies, waits for them, and re-layouts  0.66 us (6%)
    pallas_call x1, Pallas kernels, shards(): pl.pallas_call(functools.partial(kernel, count), out_shape=pltpu.VMEM(den...  10.1 us
    unnamed x1, local copies, waits for them, and re-layouts  0.66 us

profile of v2, /device:TPU:0, one launch (start us, length us, event | category | flops | bytes accessed | tf_op | source)
XLA Modules:
  0.0 10.7 jit_solution(1795091372995192209)
XLA Ops:
  0.0 10.1 %shard_map.82 = bf16[32,16,128]{2,1,0:T(8,128)(2,1)S(1)} custom-call(bf16[32,16,128]{2,1,0:T(8,128)(2,1)} %dens_hbm.1, bf16[32,8,128,128]{3,2,1,0:T(8,128)(2,1)} %near_hbm.1, s32[8,32]{1,0:T(8,128)} %bitcast.1, s32[32]{0:T(128)} %live_hbm.1, s32[32]{0:T(128)} %cmap_hbm.1, bf16[32,128,128]{2,1,0:T(8,128)(2,1)} %rest_hbm.1, bf16[32,128,128]{2,1,0:T(8,128)(2,1)} %eval_hbm.1, ...), custom_call_target="tpu_custom_call" | custom-call | tf_op jit(solution)/shard_map/pallas_call | solution.py:290
  10.1 0.7 %copy.10 = bf16[32,16,128]{2,1,0:T(8,128)(2,1)} copy(bf16[32,16,128]{2,1,0:T(8,128)(2,1)S(1)} %shard_map.82) | data formatting | bytes 262144

commit v3 on v2

--- a/solution.py
+++ b/solution.py
@@ -8,6 +8,7 @@
 from jax.sharding import PartitionSpec as P
 
 PARTS = 4
+REST_PARTS = 2
 CONTRACT_LAST = (((1,), (1,)), ((), ()))
 
 
@@ -21,6 +22,7 @@
     chips = count // 2
     last = chips - 1
     part = blk_count // PARTS
+    rest_part = blk_count // REST_PARTS
     me = lax.axis_index("panel")
     core = lax.rem(me, 2)
     chip = me // 2
@@ -41,7 +43,7 @@
         eval_copy = pltpu.make_async_copy(eval_hbm, evl, in_sem.at[5])
 
         def rest_copy(i):
-            blocks = pl.ds(i * part, part)
+            blocks = pl.ds(i * rest_part, rest_part)
             return pltpu.make_async_copy(rest_hbm.at[blocks], rest.at[blocks], rest_sem.at[i])
 
         def near_copy(i):
@@ -50,12 +52,8 @@
 
         dens_copy.start()
         cmap_copy.start()
-        for i in range(PARTS):
+        for i in range(REST_PARTS):
             rest_copy(i).start()
-        high_copy.start()
-        neigh_copy.start()
-        live_copy.start()
-        coup_copy.start()
 
         barrier = pltpu.get_barrier_semaphore()
 
@@ -83,26 +81,25 @@
         def _():
             high[pl.ds(blk_count, reach)] = jnp.zeros((reach,) + high.shape[1:], high.dtype)
 
-        @pl.when(has_low)
-        def _():
+        def meet():
             pl.semaphore_wait(barrier, me)
+
+        def reply(signal):
             pl.semaphore_signal(next_ready, inc=1, device_id={"panel": me - 1})
-
-        @pl.when(chip < last)
-        def _():
-            lax.fori_loop(0, me, answer, 0)
-
-        @pl.when(chip == last)
-        def _():
-            lax.fori_loop(0, me, answer_last, 0)
+            lax.fori_loop(0, me, signal, 0)
+
+        @pl.when(has_low & (chip < last))
+        def _():
+            meet()
+            reply(answer)
 
         dens_copy.wait()
         cmap_copy.wait()
         for b in range(blk_count):
             own = cmap[b] - me * coarse_dev
-            values = low[reach + b].astype(jnp.float32)
-            rows = [values * (own == c).astype(jnp.float32) for c in range(coarse_dev)]
-            masked[b] = jnp.concatenate(rows, axis=0).astype(jnp.bfloat16)
+            values = low[reach + b]
+            masked[b] = jnp.concatenate(
+                [jnp.where(own == c, values, jnp.zeros_like(values)) for c in range(coarse_dev)], axis=0)
 
         def halo(up):
             return pltpu.make_async_remote_copy(
@@ -116,14 +113,19 @@
             halo(False).start()
 
         total = jnp.zeros((coarse_dev * columns, rest.shape[1]), jnp.float32)
-        for i in range(PARTS):
+        for i in range(REST_PARTS):
             rest_copy(i).wait()
-            blocks = range(i * part, (i + 1) * part)
+            blocks = range(i * rest_part, (i + 1) * rest_part)
             values = jnp.concatenate([masked[b] for b in blocks], axis=1)
             weights = jnp.concatenate([rest[b] for b in blocks], axis=1)
             total += lax.dot_general(values, weights, CONTRACT_LAST, preferred_element_type=jnp.float32)
         moments[me] = total.reshape(moments.shape[1:]).astype(jnp.bfloat16)
 
+        high_copy.start()
+        neigh_copy.start()
+        live_copy.start()
+        coup_copy.start()
+
         def moment_copy(target, recv_sem):
             return pltpu.make_async_remote_copy(
                 src_ref=moments.at[me], dst_ref=moments.at[me], send_sem=send_sem, recv_sem=recv_sem,
@@ -137,13 +139,25 @@
             moment_copy(t, late_recv).start()
             return carry
 
-        @pl.when(chip < last)
-        def _():
-            lax.fori_loop(0, me, send, 0)
+        def send_down(first, stop):
+            @pl.when(chip < last)
+            def _():
+                lax.fori_loop(first, stop, send, 0)
+
+            @pl.when(chip == last)
+            def _():
+                lax.fori_loop(first, stop, send_late, 0)
 
         @pl.when(chip == last)
         def _():
-            lax.fori_loop(0, me, send_late, 0)
+            meet()
+
+        send_down(0, jnp.minimum(me, 2))
+
+        @pl.when(chip == last)
+        def _():
+            reply(answer_last)
+
 
         @pl.when(chip >= last - 1)
         def _():
@@ -158,20 +172,27 @@
             pl.semaphore_wait(next_ready, 1)
             halo(True).start()
 
-        @pl.when(me < count - 3)
-        def _():
-            pl.semaphore_wait(ready, count - 3 - me)
-            lax.fori_loop(me + 1, count - 2, send, 0)
-
-        @pl.when(chip < last)
-        def _():
-            pl.semaphore_wait(last_ready, 2)
-            lax.fori_loop(count - 2, count, send, 0)
-
-        @pl.when(me == count - 2)
-        def _():
-            pl.semaphore_wait(last_ready, 1)
-            send_late(count - 1, 0)
+        send_down(2, me)
+
+        def send_up():
+            @pl.when(me < count - 3)
+            def _():
+                pl.semaphore_wait(ready, count - 3 - me)
+                lax.fori_loop(me + 1, count - 2, send, 0)
+
+            @pl.when(chip < last)
+            def _():
+                pl.semaphore_wait(last_ready, 2)
+                lax.fori_loop(count - 2, count, send, 0)
+
+            @pl.when(me == count - 2)
+            def _():
+                pl.semaphore_wait(last_ready, 1)
+                send_late(count - 1, 0)
+
+        @pl.when(chip > 0)
+        def _():
+            send_up()
 
         neigh_copy.wait()
         live_copy.wait()
@@ -210,11 +231,21 @@
         @pl.when(core == 1)
         def _():
             low_half()
+
+        @pl.when(core == 0)
+        def _():
             high_half()
 
+        @pl.when(chip == 0)
+        def _():
+            send_up()
+
+        @pl.when(core == 1)
+        def _():
+            high_half()
+
         @pl.when(core == 0)
         def _():
-            high_half()
             low_half()
 
         coup_copy.wait()
@@ -231,7 +262,7 @@
         bytes_of(count - 1, send_sem).wait()
 
     dma = pltpu.SemaphoreType.DMA
-    pl.run_scoped(gather, dma((7,)), dma((PARTS,)), dma((PARTS,)), dma((2,)), dma)
+    pl.run_scoped(gather, dma((7,)), dma((REST_PARTS,)), dma((PARTS,)), dma((2,)), dma)
 
     @pl.when(chip < last)
     def _():

time: 10.9 us -> 10.6 us (0.972)
  Pallas kernels: 10.1 us -> 9.83 us
    pallas_call x1, Pallas kernels: 10.1 us -> 9.83 us  [shards(): pl.pallas_call(functools.partial(kernel, count), out_shape=pltpu.VMEM(den...]
where the time goes in v3:
time: 10.6 us; the launch traced here: 10.5 us
  Pallas kernels  9.83 us (93%)
  local copies, waits for them, and re-layouts  0.66 us (6%)
    pallas_call x1, Pallas kernels, shards(): pl.pallas_call(functools.partial(kernel, count), out_shape=pltpu.VMEM(den...  9.83 us
    unnamed x1, local copies, waits for them, and re-layouts  0.66 us

profile of v3, /device:TPU:0, one launch (start us, length us, event | category | flops | bytes accessed | tf_op | source)
XLA Modules:
  0.0 10.5 jit_solution(3293804194721745702)
XLA Ops:
  0.0 9.8 %shard_map.82 = bf16[32,16,128]{2,1,0:T(8,128)(2,1)S(1)} custom-call(bf16[32,16,128]{2,1,0:T(8,128)(2,1)} %dens_hbm.1, bf16[32,8,128,128]{3,2,1,0:T(8,128)(2,1)} %near_hbm.1, s32[8,32]{1,0:T(8,128)} %bitcast.1, s32[32]{0:T(128)} %live_hbm.1, s32[32]{0:T(128)} %cmap_hbm.1, bf16[32,128,128]{2,1,0:T(8,128)(2,1)} %rest_hbm.1, bf16[32,128,128]{2,1,0:T(8,128)(2,1)} %eval_hbm.1, ...), custom_call_target="tpu_custom_call" | custom-call | tf_op jit(solution)/shard_map/pallas_call | solution.py:321
  9.8 0.7 %copy.10 = bf16[32,16,128]{2,1,0:T(8,128)(2,1)} copy(bf16[32,16,128]{2,1,0:T(8,128)(2,1)S(1)} %shard_map.82) | data formatting | bytes 262144

commit v4 on v3

--- a/solution.py
+++ b/solution.py
@@ -13,7 +13,7 @@
 
 
 def kernel(count, dens_hbm, near_hbm, neigh_hbm, live_hbm, cmap_hbm, rest_hbm, eval_hbm, coup_hbm, out, neigh, live,
-           cmap, coup, low, high, near, rest, evl, masked, moments, acc, halo_recv, early_recv, late_recv, next_ready, ready, last_ready):
+           cmap, coup, low, high, near, rest, evl, masked, moments, acc, late_recv):
     slots, blk_count = neigh.shape
     reach = blk_count // 2
     columns, panels = low.shape[1:]
@@ -33,7 +33,7 @@
         block = moments.at[pl.ds(0, n)]
         return pltpu.make_async_copy(block, block, sem)
 
-    def gather(in_sem, rest_sem, near_sem, halo_send, send_sem):
+    def gather(in_sem, rest_sem, near_sem, halo_send, send_sem, halo_recv, early_recv, next_ready, ready, last_ready):
         dens_copy = pltpu.make_async_copy(dens_hbm, low.at[pl.ds(reach, blk_count)], in_sem.at[0])
         high_copy = pltpu.make_async_copy(dens_hbm, high.at[pl.ds(0, blk_count)], in_sem.at[6])
         cmap_copy = pltpu.make_async_copy(cmap_hbm, cmap, in_sem.at[1])
@@ -261,16 +261,17 @@
 
         bytes_of(count - 1, send_sem).wait()
 
-    dma = pltpu.SemaphoreType.DMA
-    pl.run_scoped(gather, dma((7,)), dma((REST_PARTS,)), dma((PARTS,)), dma((2,)), dma)
-
-    @pl.when(chip < last)
-    def _():
-        bytes_of(count - 3, early_recv).wait()
-
-    @pl.when(chip == last)
-    def _():
-        bytes_of(count - 2, early_recv).wait()
+        @pl.when(chip < last)
+        def _():
+            bytes_of(count - 3, early_recv).wait()
+
+        @pl.when(chip == last)
+        def _():
+            bytes_of(count - 2, early_recv).wait()
+
+    dma, signal = pltpu.SemaphoreType.DMA, pltpu.SemaphoreType.REGULAR
+    pl.run_scoped(gather, dma((7,)), dma((REST_PARTS,)), dma((PARTS,)), dma((2,)), dma, dma((2,)), dma,
+                  signal, signal, signal)
 
     sums = [jnp.zeros(moments.shape[2:], jnp.float32) for _ in range(coarse_dev)]
 
@@ -336,12 +337,7 @@
             pltpu.VMEM((blk_count, coarse_dev * columns, panels), jnp.bfloat16),
             pltpu.VMEM((count, coarse_dev, columns, terms), jnp.bfloat16),
             pltpu.VMEM(density.shape, jnp.float32),
-            dma((2,)),
             dma,
-            dma,
-            pltpu.SemaphoreType.REGULAR,
-            pltpu.SemaphoreType.REGULAR,
-            pltpu.SemaphoreType.REGULAR,
         ],
         compiler_params=pltpu.CompilerParams(collective_id=0, has_side_effects=True),
     )(density, near_blocks, neighbours.T, counts, coarse_map, restrict, evaluate, coupling)

time: 10.6 us -> 10.6 us (level)
  no operation moved by 1% of the time
where the time goes in v4:
time: 10.6 us; the launch traced here: 10.4 us
  Pallas kernels  9.78 us (92%)
  local copies, waits for them, and re-layouts  0.66 us (6%)
    pallas_call x1, Pallas kernels, shards(): pl.pallas_call(functools.partial(kernel, count), out_shape=pltpu.VMEM(den...  9.78 us
    unnamed x1, local copies, waits for them, and re-layouts  0.66 us

profile of v4, /device:TPU:0, one launch (start us, length us, event | category | flops | bytes accessed | tf_op | source)
XLA Modules:
  0.0 10.4 jit_solution(3602164994887544017)
XLA Ops:
  0.0 9.8 %shard_map.82 = bf16[32,16,128]{2,1,0:T(8,128)(2,1)S(1)} custom-call(bf16[32,16,128]{2,1,0:T(8,128)(2,1)} %dens_hbm.1, bf16[32,8,128,128]{3,2,1,0:T(8,128)(2,1)} %near_hbm.1, s32[8,32]{1,0:T(8,128)} %bitcast.1, s32[32]{0:T(128)} %live_hbm.1, s32[32]{0:T(128)} %cmap_hbm.1, bf16[32,128,128]{2,1,0:T(8,128)(2,1)} %rest_hbm.1, bf16[32,128,128]{2,1,0:T(8,128)(2,1)} %eval_hbm.1, ...), custom_call_target="tpu_custom_call" | custom-call | tf_op jit(solution)/shard_map/pallas_call | solution.py:322
  9.8 0.7 %copy.10 = bf16[32,16,128]{2,1,0:T(8,128)(2,1)} copy(bf16[32,16,128]{2,1,0:T(8,128)(2,1)S(1)} %shard_map.82) | data formatting | bytes 262144

commit v5 on v4

--- a/solution.py
+++ b/solution.py
@@ -8,12 +8,12 @@
 from jax.sharding import PartitionSpec as P
 
 PARTS = 4
-REST_PARTS = 2
+REST_CUTS = (0, 12, 32)
 CONTRACT_LAST = (((1,), (1,)), ((), ()))
 
 
 def kernel(count, dens_hbm, near_hbm, neigh_hbm, live_hbm, cmap_hbm, rest_hbm, eval_hbm, coup_hbm, out, neigh, live,
-           cmap, coup, low, high, near, rest, evl, masked, moments, acc, late_recv):
+           cmap, coup, low, high, near, rest, evl, masked, partial, moments, acc, late_recv):
     slots, blk_count = neigh.shape
     reach = blk_count // 2
     columns, panels = low.shape[1:]
@@ -22,7 +22,8 @@
     chips = count // 2
     last = chips - 1
     part = blk_count // PARTS
-    rest_part = blk_count // REST_PARTS
+    cuts = [blk_count * cut // 32 for cut in REST_CUTS]
+    rest_parts = len(cuts) - 1
     me = lax.axis_index("panel")
     core = lax.rem(me, 2)
     chip = me // 2
@@ -43,7 +44,7 @@
         eval_copy = pltpu.make_async_copy(eval_hbm, evl, in_sem.at[5])
 
         def rest_copy(i):
-            blocks = pl.ds(i * rest_part, rest_part)
+            blocks = pl.ds(cuts[i], cuts[i + 1] - cuts[i])
             return pltpu.make_async_copy(rest_hbm.at[blocks], rest.at[blocks], rest_sem.at[i])
 
         def near_copy(i):
@@ -52,7 +53,7 @@
 
         dens_copy.start()
         cmap_copy.start()
-        for i in range(REST_PARTS):
+        for i in range(rest_parts):
             rest_copy(i).start()
 
         barrier = pltpu.get_barrier_semaphore()
@@ -112,13 +113,20 @@
         def _():
             halo(False).start()
 
-        total = jnp.zeros((coarse_dev * columns, rest.shape[1]), jnp.float32)
-        for i in range(REST_PARTS):
+        def terms_of(i):
             rest_copy(i).wait()
-            blocks = range(i * rest_part, (i + 1) * rest_part)
+            blocks = range(cuts[i], cuts[i + 1])
             values = jnp.concatenate([masked[b] for b in blocks], axis=1)
             weights = jnp.concatenate([rest[b] for b in blocks], axis=1)
-            total += lax.dot_general(values, weights, CONTRACT_LAST, preferred_element_type=jnp.float32)
+            return lax.dot_general(values, weights, CONTRACT_LAST, preferred_element_type=jnp.float32)
+
+        partial[...] = jnp.zeros(partial.shape, partial.dtype)
+        for i in range(rest_parts - 1):
+            @pl.when(me >= 0)
+            def _(i=i):
+                partial[...] += terms_of(i)
+
+        total = partial[...] + terms_of(rest_parts - 1)
         moments[me] = total.reshape(moments.shape[1:]).astype(jnp.bfloat16)
 
         high_copy.start()
@@ -151,12 +159,13 @@
         @pl.when(chip == last)
         def _():
             meet()
-
-        send_down(0, jnp.minimum(me, 2))
-
-        @pl.when(chip == last)
-        def _():
+            send_late(0, 0)
+            send_late(1, 0)
             reply(answer_last)
+
+        @pl.when(chip < last)
+        def _():
+            lax.fori_loop(0, jnp.minimum(me, 2), send, 0)
 
 
         @pl.when(chip >= last - 1)
@@ -270,19 +279,23 @@
             bytes_of(count - 2, early_recv).wait()
 
     dma, signal = pltpu.SemaphoreType.DMA, pltpu.SemaphoreType.REGULAR
-    pl.run_scoped(gather, dma((7,)), dma((REST_PARTS,)), dma((PARTS,)), dma((2,)), dma, dma((2,)), dma,
+    pl.run_scoped(gather, dma((7,)), dma((rest_parts,)), dma((PARTS,)), dma((2,)), dma, dma((2,)), dma,
                   signal, signal, signal)
 
     sums = [jnp.zeros(moments.shape[2:], jnp.float32) for _ in range(coarse_dev)]
 
-    def add(s):
+    def weights_of(s):
+        return [[coup[c, s * coarse_dev + i] for c in range(coarse_dev)] for i in range(coarse_dev)]
+
+    def add(s, factors):
         for i in range(coarse_dev):
             term = moments[s, i].astype(jnp.float32)
             for c in range(coarse_dev):
-                sums[c] += coup[c, s * coarse_dev + i] * term
+                sums[c] += factors[i][c] * term
 
     for s in range(count - 2):
-        add(s)
+        add(s, weights_of(s))
+    late_factors = [weights_of(s) for s in (count - 2, count - 1)]
 
     @pl.when(chip < last)
     def _():
@@ -292,8 +305,8 @@
     def _():
         bytes_of(1, late_recv).wait()
 
-    add(count - 2)
-    add(count - 1)
+    add(count - 2, late_factors[0])
+    add(count - 1, late_factors[1])
     spread = [total.astype(jnp.bfloat16) for total in sums]
     blank = jnp.zeros_like(spread[0])
     lhs = jnp.concatenate([jnp.concatenate([e, blank], axis=1) for e in spread]
@@ -335,6 +348,7 @@
             pltpu.VMEM(restrict.shape, jnp.bfloat16),
             pltpu.VMEM(evaluate.shape, jnp.bfloat16),
             pltpu.VMEM((blk_count, coarse_dev * columns, panels), jnp.bfloat16),
+            pltpu.VMEM((coarse_dev * columns, terms), jnp.float32),
             pltpu.VMEM((count, coarse_dev, columns, terms), jnp.bfloat16),
             pltpu.VMEM(density.shape, jnp.float32),
             dma,

time: 10.6 us -> 10.5 us (level)
  no operation moved by 1% of the time
where the time goes in v5:
time: 10.5 us; the launch traced here: 10.4 us
  Pallas kernels  9.7 us (92%)
  local copies, waits for them, and re-layouts  0.66 us (6%)
    pallas_call x1, Pallas kernels, shards(): pl.pallas_call(functools.partial(kernel, count), out_shape=pltpu.VMEM(den...  9.7 us
    unnamed x1, local copies, waits for them, and re-layouts  0.66 us

profile of v5, /device:TPU:0, one launch (start us, length us, event | category | flops | bytes accessed | tf_op | source)
XLA Modules:
  0.0 10.4 jit_solution(2674484746414023613)
XLA Ops:
  0.0 9.7 %shard_map.82 = bf16[32,16,128]{2,1,0:T(8,128)(2,1)S(1)} custom-call(bf16[32,16,128]{2,1,0:T(8,128)(2,1)} %dens_hbm.1, bf16[32,8,128,128]{3,2,1,0:T(8,128)(2,1)} %near_hbm.1, s32[8,32]{1,0:T(8,128)} %bitcast.1, s32[32]{0:T(128)} %live_hbm.1, s32[32]{0:T(128)} %cmap_hbm.1, bf16[32,128,128]{2,1,0:T(8,128)(2,1)} %rest_hbm.1, bf16[32,128,128]{2,1,0:T(8,128)(2,1)} %eval_hbm.1, ...), custom_call_target="tpu_custom_call" | custom-call | tf_op jit(solution)/shard_map/pallas_call | solution.py:335
  9.7 0.7 %copy.10 = bf16[32,16,128]{2,1,0:T(8,128)(2,1)} copy(bf16[32,16,128]{2,1,0:T(8,128)(2,1)S(1)} %shard_map.82) | data formatting | bytes 262144

commit v6 on v5

--- a/solution.py
+++ b/solution.py
@@ -51,9 +51,10 @@
             blocks = pl.ds(i * part, part)
             return pltpu.make_async_copy(near_hbm.at[blocks], near.at[blocks], near_sem.at[i])
 
+        rest_copy(0).start()
         dens_copy.start()
         cmap_copy.start()
-        for i in range(rest_parts):
+        for i in range(1, rest_parts):
             rest_copy(i).start()
 
         barrier = pltpu.get_barrier_semaphore()

time: 10.5 us -> 10.6 us (level)
  no operation moved by 1% of the time
where the time goes in v6:
time: 10.6 us; the launch traced here: 10.4 us
  Pallas kernels  9.76 us (92%)
  local copies, waits for them, and re-layouts  0.66 us (6%)
    pallas_call x1, Pallas kernels, shards(): pl.pallas_call(functools.partial(kernel, count), out_shape=pltpu.VMEM(den...  9.76 us
    unnamed x1, local copies, waits for them, and re-layouts  0.66 us

profile of v6, /device:TPU:0, one launch (start us, length us, event | category | flops | bytes accessed | tf_op | source)
XLA Modules:
  0.0 10.4 jit_solution(4555102999029329556)
XLA Ops:
  0.0 9.8 %shard_map.82 = bf16[32,16,128]{2,1,0:T(8,128)(2,1)S(1)} custom-call(bf16[32,16,128]{2,1,0:T(8,128)(2,1)} %dens_hbm.1, bf16[32,8,128,128]{3,2,1,0:T(8,128)(2,1)} %near_hbm.1, s32[8,32]{1,0:T(8,128)} %bitcast.1, s32[32]{0:T(128)} %live_hbm.1, s32[32]{0:T(128)} %cmap_hbm.1, bf16[32,128,128]{2,1,0:T(8,128)(2,1)} %rest_hbm.1, bf16[32,128,128]{2,1,0:T(8,128)(2,1)} %eval_hbm.1, ...), custom_call_target="tpu_custom_call" | custom-call | tf_op jit(solution)/shard_map/pallas_call | solution.py:336
  9.8 0.7 %copy.10 = bf16[32,16,128]{2,1,0:T(8,128)(2,1)} copy(bf16[32,16,128]{2,1,0:T(8,128)(2,1)S(1)} %shard_map.82) | data formatting | bytes 262144
